TPU v7x, 32 devices: a whole 2x2x4 slice. The times are simulated.
32 devices in a mesh: sector: 2 (over y), term: 16 (over z, x, core).
Axes of the slice: x: 2, y: 2, z: 4, core: 2. Of those that a mesh axis runs over, the one named last changes fastest.
Arguments:
- wave_in: bfloat16 [16, 1024, 256], P('sector'), may hold values from -6 to 6
- left_env: bfloat16 [16, 192, 1024, 256], P('sector', 'term'), may hold values from -0.1875 to 0.1875
- right_env: bfloat16 [16, 192, 256, 64], P('sector', 'term'), may hold values from -0.375 to 0.375
- shift_map: int32 [48, 16], replicated, may hold values from 0 to 15
- live_rows: int32 [16], replicated, may hold values from 512 to 1024
Outputs:
- isometry: bfloat16 [16, 1024, 256], P('sector', 'term')
- env_next: bfloat16 [16, 192, 256, 64], P('sector', 'term')
All inputs are finite; a program needn't handle non-finite values.
Results may differ from a plain program's by a relative error of at most 0.014.
Values may be sent and summed in bfloat16 or wider, within the bound.
No kernel may reach another device: no remote copies, remote signals or barrier semaphores. Data moves between devices by JAX's collectives and lax.ppermute only.
A program may use at most 192 MiB of HBM per device.

v0:
```python
import math

import jax
import jax.numpy as jnp
from jax import lax
from jax.sharding import PartitionSpec as P

STEPS = 8


step_size = 0.15
epsilon = 1e-06
highest = lax.Precision.HIGHEST


def from_partner(block, axis, bit):
    count = lax.axis_size(axis)
    route = []
    for low in range(count):
        high = low | 1 << bit
        if high != low and high < count:
            route += [(low, high), (high, low)]
    return lax.ppermute(block, axis, route)


def body(wave_in, left_env, right_env, shift_map, live_rows):
    sec_dev, width_left, width_right = wave_in.shape
    pair_dev = left_env.shape[1]
    slices = width_left // left_env.shape[3]
    left_part = width_left // slices
    levels = slices.bit_length() - 1
    term_pos = lax.axis_index("term")
    slice_pos = term_pos % slices
    group_pos = term_pos // slices
    first_sector = lax.axis_index("sector") * sec_dev
    blocks = right_env[:, :, :, None, :]
    for bit_level in range(levels):
        partner = from_partner(blocks, "term", bit_level)
        upper_half = slice_pos // 2**bit_level % 2 == 1
        blocks = jnp.concatenate(
            [jnp.where(upper_half, partner, blocks), jnp.where(upper_half, blocks, partner)], axis=3
        )
    right_complete = blocks.reshape(sec_dev, pair_dev, width_right, width_right)
    terms_here = lax.dynamic_slice_in_dim(shift_map, group_pos * pair_dev, pair_dev, 0)
    sources = lax.dynamic_slice_in_dim(terms_here, first_sector, sec_dev, 1).T
    limits = lax.dynamic_slice_in_dim(live_rows, first_sector, sec_dev, 0)
    mine_rows = lax.dynamic_slice_in_dim(wave_in, slice_pos * left_part, left_part, 1)
    every_rows = lax.all_gather(mine_rows, "sector", axis=0, tiled=True)
    selected_block = every_rows[sources]
    operator_applied = jnp.einsum(
        "spab,spbc->spac", selected_block, right_complete, preferred_element_type=jnp.float32
    ).astype(jnp.bfloat16)
    row_share = width_left // lax.axis_size("term")
    term_total = jnp.einsum(
        "spia,spac->sic", left_env, operator_applied, preferred_element_type=jnp.float32
    )
    sigma_block_sum = lax.psum(term_total, "term")
    row_total = sigma_block_sum.shape[1]
    own_rows = wave_in.astype(jnp.float32)
    row_index = jnp.arange(row_total, dtype=jnp.int32)
    live_mask = row_index[None, :, None] < limits[:, None, None]
    updated = jnp.where(live_mask, own_rows - step_size * sigma_block_sum, 0.0)
    gram_sum = jnp.einsum("sia,sib->sab", updated, updated, precision=highest)
    trace_sum = jnp.trace(gram_sum, axis1=1, axis2=2) + epsilon
    identity = jnp.eye(width_right, dtype=jnp.float32)
    root_part = gram_sum / trace_sum[:, None, None]
    inverse_part = jnp.broadcast_to(identity, root_part.shape)
    for ns_step in range(STEPS):
        ns_factor = 1.5 * identity - 0.5 * jnp.einsum(
            "sab,sbc->sac", inverse_part, root_part, precision=highest
        )
        root_part = jnp.einsum("sab,sbc->sac", root_part, ns_factor, precision=highest)
        inverse_part = jnp.einsum("sab,sbc->sac", ns_factor, inverse_part, precision=highest)
    result = (
        jnp.einsum("sia,sab->sib", updated, inverse_part, precision=highest)
        * jnp.sqrt(width_left / trace_sum)[:, None, None]
    )
    wave_rows = result.astype(jnp.bfloat16)
    wave_out = lax.dynamic_slice_in_dim(wave_rows, term_pos * row_share, row_share, 1)
    source_rows = lax.dynamic_slice_in_dim(wave_rows, slice_pos * left_part, left_part, 1)
    every_source = lax.all_gather(source_rows, "sector", axis=0, tiled=True)
    picked_wave = every_source[sources]
    projected_wave = jnp.einsum(
        "sia,spib->spab", wave_rows, left_env, preferred_element_type=jnp.float32
    ).astype(jnp.bfloat16)
    partial_value = jnp.einsum(
        "spab,spbc->spac", projected_wave, picked_wave, preferred_element_type=jnp.float32
    )
    blocks = partial_value.reshape(sec_dev, pair_dev, width_right, slices, width_right // slices)
    for bit_level in reversed(range(levels)):
        half_count = blocks.shape[3] // 2
        upper_half = slice_pos // 2**bit_level % 2 == 1
        low_half = blocks[:, :, :, :half_count]
        high_half = blocks[:, :, :, half_count:]
        kept_half = jnp.where(upper_half, high_half, low_half)
        sent_half = jnp.where(upper_half, low_half, high_half)
        blocks = kept_half + from_partner(sent_half.astype(jnp.bfloat16), "term", bit_level).astype(
            sent_half.dtype
        )
    environment_block = (blocks[:, :, :, 0] / math.sqrt(width_left)).astype(jnp.bfloat16)
    return (wave_out, environment_block)


def solution(mesh):
    in_specs = (
        P("sector", None, None),
        P("sector", "term", None, None),
        P("sector", "term", None, None),
        P(),
        P(),
    )
    out_specs = (P("sector", "term", None), P("sector", "term", None, None))
    return jax.shard_map(body, mesh=mesh, in_specs=in_specs, out_specs=out_specs, check_vma=False)
```

profile of v0, /device:TPU:0, one launch (start us, length us, event | category | flops | bytes accessed | tf_op | source)
XLA Modules:
  0.0 711.1 jit_solution(4461053631393989367)
XLA Ops:
  7.8 5.6 collective-permute-done
  13.4 3.3 broadcast_select_fusion.3
  16.7 3.6 pad_maximum_fusion.1
  20.3 2.8 collective-permute-start.1
  25.8 33.3 %all-gather.3.cloned.1.call-done = bf16[16,256,256]{2,1,0:T(8,128)(2,1)} async-done(((bf16[8,256,256]{2,1,0:T(8,128)(2,1)}), bf16[16,256,256]{2,1,0:T(8,128)(2,1)}) %all-gather.3.cloned.1.call-update) | async-done | bytes 2097168 | tf_op jit(solution)/shard_map/all_gather | solution.py:48
  59.0 8.4 %gather_fusion = bf16[96,256,256]{2,1,0:T(8,128)(2,1)} fusion(bf16[16,256,256]{2,1,0:T(8,128)(2,1)} %all-gather.3.cloned.1.call-done, s32[1024]{0:T(1024)S(1)} %pad_clamp_fusion), kind=kCustom, calls=%fused_computation | custom fusion | bytes 25166208 | tf_op jit(solution)/shard_map/gather | solution.py:49
  67.4 91.8 %collective-permute-done.1 = bf16[8,12,256,2,64]{2,4,3,1,0:T(8,128)(2,1)} collective-permute-done((bf16[8,12,256,2,64]{2,4,3,1,0:T(8,128)(2,1)}, bf16[8,12,256,2,64]{2,4,3,1,0:T(8,128)(2,1)}, u32[]{:S(2)}, u32[]{:S(2)}) %collective-permute-start.1) | collective-permute-done | bytes 6291488 | tf_op jit(solution)/shard_map/ppermute | solution.py:23
  159.3 4.5 broadcast_select_fusion.1
  163.7 5.2 pad_maximum_fusion
  168.9 30.8 %fusion.19 = f32[8,1024,256]{1,2,0:T(8,128)} fusion(bf16[8,12,1024,256]{3,2,1,0:T(8,128)(2,1)} %param.6, bf16[8,12,256,256]{3,2,1,0:T(8,128)(2,1)} %bitcast.73, bf16[8,12,256,256]{2,3,1,0:T(8,128)(2,1)} %bitcast.72), kind=kOutput, calls=%fused_computation.28 | convolution fusion | flops 16112418816 | bytes 83886080 | tf_op jit(solution)/shard_map/spia,spac->sic/dot_general | solution.py:54
  200.3 6.5 copy.17
  207.0 164.4 %all-reduce.2.cloned.1.call-done = f32[8,1024,256]{1,2,0:T(8,128)} async-done(((f32[8,1024,256]{1,2,0:T(8,128)}), f32[8,1024,256]{1,2,0:T(8,128)}) %all-reduce.2.cloned.1.call-update) | async-done | bytes 8388624 | tf_op jit(solution)/shard_map/psum | solution.py:57
  371.4 26.7 %select_reduce_fusion = (f32[8]{0:T(128)S(1)}, f32[8,256,256]{2,1,0:T(8,128)S(1)}) fusion(pred[256,256]{1,0:T(8,128)(4,1)S(1)} %iota_compare_fusion, f32[8,1024,256]{1,2,0:T(8,128)} %all-reduce.2.cloned.1.call-done, bf16[8,1024,256]{1,2,0:T(8,128)(2,1)} %copy.17, pred[8,1024]{1,0:T(8,128)(4,1)S(1)} %iota_compare_fusion.1), kind=kOutput, calls=%fused_computation.42 | convolution fusion | flops 6451888128 | bytes 14753824 | tf_op jit(solution)/shard_map/sia,sib->sab/dot_general | solution.py:63
  451.0 14.3 %multiply_convert_fusion = bf16[8,1024,256]{2,1,0:T(8,128)(2,1)S(1)} fusion(f32[8]{0:T(128)S(1)} %get-tuple-element.7, f32[8,256,256]{2,1,0:T(8,128)S(1)} %fusion.23, f32[8,1024,256]{1,2,0:T(8,128)S(1)} %bitcast.75, bf16[8,1024,256]{1,2,0:T(8,128)(2,1)S(1)} %copy-done.2, pred[8,1024]{1,0:T(8,128)(4,1)S(1)} %iota_compare_fusion.1), kind=kOutput, calls=%fused_computation.11 | convolution fusion | flops 6455033856 | bytes 18882592 | tf_op jit(solution)/shard_map/sia,sab->sib/dot_general | solution.py:75
  468.5 25.7 %fusion.143 = bf16[8,12,256,256]{3,2,1,0:T(8,128)(2,1)} fusion(bf16[8,12,1024,256]{3,2,1,0:T(8,128)(2,1)} %param.6, bf16[8,1024,256]{2,1,0:T(8,128)(2,1)} %copy-done.3), kind=kOutput, calls=%fused_computation.4.clone.1 | convolution fusion | flops 12891193344 | bytes 67108864 | tf_op jit(solution)/shard_map/sia,spib->spab/dot_general | solution.py:83
  494.2 7.4 %all-gather.5.cloned.1.call-done = bf16[16,256,256]{2,1,0:T(8,128)(2,1)} async-done(((bf16[8,256,256]{2,1,0:T(8,128)(2,1)}), bf16[16,256,256]{2,1,0:T(8,128)(2,1)}) %all-gather.5.cloned.1.call-update) | async-done | bytes 2097168 | tf_op jit(solution)/shard_map/all_gather | solution.py:81
  501.6 8.5 %gather_fusion.1 = bf16[96,256,256]{2,1,0:T(8,128)(2,1)} fusion(bf16[16,256,256]{2,1,0:T(8,128)(2,1)} %all-gather.5.cloned.1.call-done, s32[1024]{0:T(1024)S(1)} %copy-done.5), kind=kCustom, calls=%fused_computation.1 | custom fusion | bytes 25166208 | tf_op jit(solution)/shard_map/gather | solution.py:82
  510.1 19.0 %fusion = f32[8,12,256,256]{2,3,1,0:T(8,128)} fusion(bf16[8,12,256,256]{3,2,1,0:T(8,128)(2,1)} %bitcast.71, bf16[8,12,256,256]{3,2,1,0:T(8,128)(2,1)} %fusion.143), kind=kOutput, calls=%fused_computation.3 | convolution fusion | flops 3221225472 | bytes 50331648 | tf_op jit(solution)/shard_map/spab,spbc->spac/dot_general | solution.py:86
  529.1 8.9 %select_convert_fusion = bf16[8,12,256,2,64]{2,4,3,1,0:T(8,128)(2,1)S(1)} fusion(f32[8,12,256,4,64]{2,4,3,1,0:T(8,128)} %bitcast.69, pred[]{:T(512)S(6)} %eq.43), kind=kLoop, calls=%fused_computation.6 | loop fusion | flops 3145728 | bytes 18874368 | tf_op jit(solution)/shard_map/convert_element_type | solution.py:97
  539.5 135.6 %collective-permute-done.2 = bf16[8,12,256,2,64]{2,4,3,1,0:T(8,128)(2,1)S(1)} collective-permute-done((bf16[8,12,256,2,64]{2,4,3,1,0:T(8,128)(2,1)S(1)}, bf16[8,12,256,2,64]{2,4,3,1,0:T(8,128)(2,1)S(1)}, u32[]{:S(2)}, u32[]{:S(2)}) %collective-permute-start.2) | collective-permute-done | bytes 6291488 | tf_op jit(solution)/shard_map/ppermute | solution.py:23
  675.1 9.8 %convert_add_fusion = f32[8,12,256,2,64]{2,4,3,1,0:T(8,128)S(1)} fusion(bf16[8,12,256,2,64]{2,4,3,1,0:T(8,128)(2,1)S(1)} %collective-permute-done.2, f32[8,12,256,4,64]{2,4,3,1,0:T(8,128)} %bitcast.70, pred[]{:T(512)S(6)} %eq.43), kind=kLoop, calls=%fused_computation.5 | loop fusion | flops 9437184 | bytes 44040192 | tf_op jit(solution)/shard_map/add | solution.py:97
  684.9 4.5 copy-done
  691.8 4.1 collective-permute-done.3
  695.9 8.2 %fusion.22 = bf16[8,12,256,64]{2,3,1,0:T(8,128)(2,1)} fusion(bf16[8,12,256,1,64]{2,4,3,1,0:T(8,128)(2,1)} %collective-permute-done.3, f32[8,12,256,2,64]{2,4,3,1,0:T(8,128)} %copy-done, pred[]{:T(512)S(6)} %eq.44), kind=kLoop, calls=%fused_computation.29 | loop fusion | flops 7864320 | bytes 18874368 | tf_op jit(solution)/shard_map/convert_element_type | solution.py:100
  (65 shorter events, 63.6 us)
Async XLA Ops:
  7.2 51.9 %all-gather.3.cloned.1.call-start = ((), (), s32[]{:S(2)}) async-start(), calls=%async_computation | async-start | bytes 3145728 | tf_op jit(solution)/shard_map/all_gather | solution.py:48
  7.2 6.2 collective-permute-start
  16.7 3.6 copy-start.1
  20.3 5.3 copy-start.6
  20.3 139.0 %collective-permute-start.1 = (bf16[8,12,256,2,64]{2,4,3,1,0:T(8,128)(2,1)}, bf16[8,12,256,2,64]{2,4,3,1,0:T(8,128)(2,1)}, u32[]{:S(2)}, u32[]{:S(2)}) collective-permute-start(bf16[8,12,256,2,64]{2,4,3,1,0:T(8,128)(2,1)} %pad_maximum_fusion.1), channel_id=1, source_target_pairs={{0,2},{2,0},{1,3},{3,1},{4,6},{6,4},{5,7},{7,5},{8,10},{10,8},{9,1... | collective-permute-start | bytes 18874376 | tf_op jit(solution)/shard_map/ppermute | solution.py:23
  25.4 346.0 %all-reduce.2.cloned.1.call-start = ((), (), s32[]{:S(2)}) async-start(), calls=%async_computation.1 | async-start | bytes 16777216 | tf_op jit(solution)/shard_map/psum | solution.py:57
  25.7 41.7 %copy-start.4 = (s32[1024]{0:T(1024)}, s32[1024]{0:T(1024)S(1)}, u32[]{:S(2)}) copy-start(s32[1024]{0:T(1024)S(1)} %pad_clamp_fusion) | copy-start | bytes 12292
  199.7 7.1 copy-start.7
  199.7 301.8 %all-gather.5.cloned.1.call-start = ((), (), s32[]{:S(2)}) async-start(), calls=%async_computation.2 | async-start | bytes 3145728 | tf_op jit(solution)/shard_map/all_gather | solution.py:81
  444.0 7.0 slice-start
  446.3 4.7 slice-start.1
  448.7 2.3 copy-start.2
  465.3 2.1 copy-start.3
  468.5 33.1 %copy-start.5 = (s32[1024]{0:T(1024)S(1)}, s32[1024]{0:T(1024)}, u32[]{:S(2)}) copy-start(s32[1024]{0:T(1024)} %copy-done.4) | copy-start | bytes 12292
  537.9 137.2 %collective-permute-start.2 = (bf16[8,12,256,2,64]{2,4,3,1,0:T(8,128)(2,1)S(1)}, bf16[8,12,256,2,64]{2,4,3,1,0:T(8,128)(2,1)S(1)}, u32[]{:S(2)}, u32[]{:S(2)}) collective-permute-start(bf16[8,12,256,2,64]{2,4,3,1,0:T(8,128)(2,1)S(1)} %select_convert_fusion), channel_id=1, source_target_pairs={{0,2},{2,0},{1,3},{3,1},{4,6},{6,4},{5,7},{7,5},{8,10},{10,8},{9,1... | collective-permute-start | bytes 18874376 | tf_op jit(solution)/shard_map/ppermute | solution.py:23
  684.9 4.5 copy-start
  690.0 5.9 collective-permute-start.3
Sparse Core Ops, SparseCore 0:
  25.6 33.4 all-gather.2
  199.8 171.5 all-reduce.1
  468.6 32.9 all-gather.4
where the time goes:
time: 716 us; the launch traced here: 711 us
  waiting for transfers between devices  442 us (62%)
  matrix products  169 us (24%)
  other arithmetic  44.2 us (6%)
  local copies, waits for them, and re-layouts  35.1 us (5%)
  between operations  14.6 us (2%)
    ppermute x4, waiting for transfers between devices, from_partner(): return lax.ppermute(block, axis, route)  237 us
    psum x1, waiting for transfers between devices, body(): sigma_block_sum = lax.psum(term_total, 'term')  164 us
    all_gather x1, waiting for transfers between devices, body(): every_rows = lax.all_gather(mine_rows, 'sector', axis=0, tiled=True)  33.3 us
    dot_general x1, matrix products, body(): jnp.einsum('spia,spac->sic', left_env, operator_applied, preferred_elemen...  30.8 us
    dot_general x1, matrix products, body(): gram_sum = jnp.einsum('sia,sib->sab', updated, updated, precision=highest)  26.7 us
    dot_general x1, matrix products, body(): jnp.einsum('sia,spib->spab', wave_rows, left_env, preferred_element_type=...  25.7 us
    dot_general x1, matrix products, body(): jnp.einsum('spab,spbc->spac', projected_wave, picked_wave, preferred_elem...  19 us
    dot_general x8, matrix products, body(): jnp.einsum('sab,sbc->sac', ns_factor, inverse_part, precision=highest)  18.4 us
  transfers between devices with their start and end apart: 7, of which 7 were waited for; matrix products, arithmetic and copies ran while one was open for 6% of the time, Pallas kernels for 0%

commit v1 on v0

v1 whole, which is shorter than its diff:
```python
import functools
import math

import jax
import jax.numpy as jnp
from jax import lax
from jax.experimental import pallas as pl
from jax.experimental.pallas import tpu as pltpu
from jax.sharding import PartitionSpec as P


STEPS = 8
step_size = 0.15
epsilon = 1e-06
f32 = jnp.float32
bf16 = jnp.bfloat16
NT = (((1,), (1,)), ((), ()))


def from_partner(block, axis, bit):
    count = lax.axis_size(axis)
    route = []
    for low in range(count):
        high = low | 1 << bit
        if high != low and high < count:
            route += [(low, high), (high, low)]
    return lax.ppermute(block, axis, route)


def divisor(count, most):
    return max(d for d in range(1, most + 1) if count % d == 0)


def aligned(index, size):
    return pl.ds(pl.multiple_of(index * size, size), size)


def dot(a, b):
    return jnp.dot(a, b, preferred_element_type=f32)


def dot_nt(a, b):
    return lax.dot_general(a, b, NT, preferred_element_type=f32)


def sigma_kernel(slices, terms, meta, idx, *refs):
    w_refs, refs = refs[:terms], refs[terms:]
    right_refs, refs = refs[:slices], refs[slices:]
    left_refs, (keep_ref, send_ref, acc, right, applied) = refs[:terms], refs[terms:]
    rows, part = left_refs[0].shape[2:]
    far, group, groups = pl.program_id(0), pl.program_id(2), pl.num_programs(2)
    me = meta[0]
    own_slice = jnp.bitwise_and(me, slices - 1)
    share = right_refs[0].shape[2]
    for j in range(terms):
        for k, ref in enumerate(right_refs):
            right[j, aligned(jnp.bitwise_xor(own_slice, k), share), :] = ref[0, j]
        applied[j * part:(j + 1) * part, :] = dot_nt(w_refs[j][0], right[j]).astype(bf16)
    tile = min(rows, 512)

    def rows_step(m, carry):
        at = aligned(m, tile)
        left = jnp.concatenate([ref[0, 0, at, :] for ref in left_refs], axis=1)
        value = dot(left, applied[...])

        @pl.when(group == 0)
        def _():
            acc[at, :] = value

        @pl.when(group > 0)
        def _():
            acc[at, :] += value

        return carry

    lax.fori_loop(0, rows // tile, rows_step, 0)
    half = rows // 2
    upper = jnp.bitwise_and(lax.div(me, slices), 1)

    def emit(out):
        for q in range(2):
            out[q, 0] = acc[aligned(jnp.bitwise_xor(upper, q), half), :].astype(bf16)

    @pl.when((group == groups - 1) & (far == 0))
    def _():
        emit(keep_ref)

    @pl.when((group == groups - 1) & (far == 1))
    def _():
        emit(send_ref)


def sigma_call(meta, idx, every_rows, rights, firsts, left_env, first, count):
    _, pair_dev, rows, part = left_env.shape
    share, width = rights[0].shape[2:]
    terms = divisor(pair_dev, 3)
    pairs = count // 2

    def at(h, i, m):
        return jnp.bitwise_xor(h, jnp.bitwise_and(m[0], 1)) * pairs + i

    def source_spec(j):
        return pl.BlockSpec(
            (1,) + every_rows.shape[1:], lambda h, i, g, m, x: (x[at(h, i, m), g * terms + j], 0, 0)
        )

    def right_spec(start):
        return pl.BlockSpec(
            (1, terms, share, width), lambda h, i, g, m, x: (at(h, i, m) + start, g, 0, 0)
        )

    def left_spec(j):
        return pl.BlockSpec(
            (1, 1, rows, part), lambda h, i, g, m, x: (at(h, i, m) + first, g * terms + j, 0, 0)
        )

    out = jax.ShapeDtypeStruct((2, pairs, rows // 2, width), bf16)
    block = (2, 1, rows // 2, width)
    return pl.pallas_call(
        functools.partial(sigma_kernel, len(rights), terms),
        out_shape=(out, out),
        grid_spec=pltpu.PrefetchScalarGridSpec(
            num_scalar_prefetch=2,
            grid=(2, pairs, pair_dev // terms),
            in_specs=[source_spec(j) for j in range(terms)]
            + [right_spec(start) for start in firsts]
            + [left_spec(j) for j in range(terms)],
            out_specs=(
                pl.BlockSpec(block, lambda h, i, g, m, x: (0, jnp.where(h == 0, i, pairs - 1), 0, 0)),
                pl.BlockSpec(block, lambda h, i, g, m, x: (0, jnp.where(h == 0, 0, i), 0, 0)),
            ),
            scratch_shapes=[
                pltpu.VMEM((rows, width), f32),
                pltpu.VMEM((terms, width, width), bf16),
                pltpu.VMEM((terms * part, width), bf16),
            ],
        ),
        cost_estimate=pl.CostEstimate(
            flops=2 * count * pair_dev * width * part * (rows + width),
            bytes_accessed=2 * count * pair_dev * rows * part,
            transcendentals=0,
        ),
        compiler_params=pltpu.CompilerParams(
            dimension_semantics=("arbitrary",) * 3, vmem_limit_bytes=40 << 20
        ),
        name="sigma",
    )(meta, idx, *[every_rows] * terms, *rights, *[left_env] * terms)


def split(a):
    high = a.astype(bf16)
    return high, (a - high.astype(f32)).astype(bf16)


def mm3(a, b):
    (ah, al), (bh, bl) = a, b
    return dot(jnp.concatenate([ah, ah, al], axis=1), jnp.concatenate([bh, bl, bh], axis=0))


def update_kernel(slices, each, meta, limits, own_ref, far_ref, wave_ref, iso_ref, rows_ref, up):
    me = meta[0]
    step = pl.program_id(0)
    half, width = own_ref.shape[1:]
    rows = wave_ref.shape[1]
    block = rows_ref.shape[2]
    ri = lax.broadcasted_iota(jnp.int32, (width, width), 0)
    ci = lax.broadcasted_iota(jnp.int32, (width, width), 1)
    eye = jnp.where(ri == ci, 1.0, 0.0).astype(f32)
    upper = jnp.bitwise_and(lax.div(me, slices), 1)
    grams, sizes, ups = [], [], []
    for n in range(each):
        limit = limits[step * each + n]
        for q, ref in enumerate((own_ref, far_ref)):
            at = jnp.bitwise_xor(upper, q)
            wave = wave_ref[n, aligned(at, half), :].astype(f32)
            live = at * half + lax.broadcasted_iota(jnp.int32, (half, width), 0) < limit
            up[n, aligned(at, half), :] = jnp.where(live, wave - step_size * ref[n].astype(f32), 0.0)
        high, low = split(up[n].T)
        cross = dot_nt(high, low)
        gram = dot_nt(high, high) + (cross + cross.T)
        size = jnp.sum(jnp.sum(gram * eye, axis=1, keepdims=True), axis=0, keepdims=True) + epsilon
        ups.append((high, low))
        grams.append(gram)
        sizes.append(size)
    roots = [gram / size for gram, size in zip(grams, sizes)]
    inverses = [None] * each
    for ns_step in range(STEPS):
        if ns_step == 0:
            products = roots
            roots = [split(root) for root in roots]
        else:
            roots = [split(root) for root in roots]
            products = [mm3(inverse, root) for inverse, root in zip(inverses, roots)]
        factors = [split(1.5 * eye - 0.5 * product) for product in products]
        if ns_step < STEPS - 1:
            roots = [mm3(root, factor) for root, factor in zip(roots, factors)]
        if ns_step == 0:
            inverses = factors
        else:
            inverses = [split(mm3(factor, inverse)) for factor, inverse in zip(factors, inverses)]
    for n in range(each):
        scale = jnp.sqrt(rows / sizes[n])
        iso_ref[n] = (mm3(inverses[n], ups[n]) * scale).astype(bf16)
        for q in range(2):
            own = split(up[n, aligned(jnp.bitwise_xor(me, q), block), :])
            rows_ref[q, n] = (mm3(own, inverses[n]) * scale).astype(bf16)


def update_call(meta, limits, own, far, wave_in, first, slices, positions):
    pairs, half, width = own.shape
    rows = wave_in.shape[1]
    each = divisor(pairs, 2)
    piece = pl.BlockSpec((each, half, width), lambda s, m, i: (s, 0, 0))
    return pl.pallas_call(
        functools.partial(update_kernel, slices, each),
        out_shape=(
            jax.ShapeDtypeStruct((pairs, width, rows), bf16),
            jax.ShapeDtypeStruct((2, pairs, rows // positions, width), bf16),
        ),
        grid_spec=pltpu.PrefetchScalarGridSpec(
            num_scalar_prefetch=2,
            grid=(pairs // each,),
            in_specs=[
                piece,
                piece,
                pl.BlockSpec(
                    (each, rows, width),
                    lambda s, m, i: (
                        s + (first + jnp.bitwise_and(m[0], 1) * pairs) // each, 0, 0
                    ),
                ),
            ],
            out_specs=(
                pl.BlockSpec((each, width, rows), lambda s, m, i: (s, 0, 0)),
                pl.BlockSpec((2, each, rows // positions, width), lambda s, m, i: (0, s, 0, 0)),
            ),
            scratch_shapes=[pltpu.VMEM((each, rows, width), f32)],
        ),
        cost_estimate=pl.CostEstimate(
            flops=pairs * (3 * 2 * width**3 * 21 + 6 * 2 * width * width * rows),
            bytes_accessed=pairs * rows * width * 8,
            transcendentals=0,
        ),
        compiler_params=pltpu.CompilerParams(
            dimension_semantics=("arbitrary",), vmem_limit_bytes=40 << 20
        ),
        name="update",
    )(meta, limits, own, far, wave_in)


def renorm_kernel(slices, terms, scale, meta, idx, iso_ref, *refs):
    part_refs, left_refs, (keep_ref, send_ref) = refs[:terms], refs[terms:2 * terms], refs[2 * terms:]
    own_slice = jnp.bitwise_and(meta[0], slices - 1)
    share = keep_ref.shape[3]
    for j in range(terms):
        front = dot(iso_ref[0], left_refs[j][0, 0]).astype(bf16)
        picked = jnp.concatenate(
            [part_refs[j][0, aligned(jnp.bitwise_xor(own_slice, k), share), :] for k in range(slices)],
            axis=0,
        )
        value = (dot_nt(picked, front) * scale).astype(bf16)
        for k in range(slices):
            out = send_ref if k % 2 else keep_ref
            out[k // 2, 0, j] = value[k * share:(k + 1) * share]


def renorm_call(meta, idx, iso, within, parts, left_env, first, slices):
    _, pair_dev, rows, part = left_env.shape
    pairs, width = iso.shape[0] // 2, iso.shape[1]
    share = width // slices
    terms = divisor(pair_dev, 3)

    def part_spec(j):
        return pl.BlockSpec((1,) + parts.shape[1:], lambda g, m, x: (x[g * terms + j], 0, 0))

    def left_spec(j):
        return pl.BlockSpec((1, 1, rows, part), lambda g, m, x: (first, g * terms + j, 0, 0))

    out = jax.ShapeDtypeStruct((slices // 2, 1, pair_dev, share, width), bf16)
    out_spec = pl.BlockSpec((slices // 2, 1, terms, share, width), lambda g, m, x: (0, 0, g, 0, 0))
    return pl.pallas_call(
        functools.partial(renorm_kernel, slices, terms, 1 / math.sqrt(rows)),
        out_shape=(out, out),
        grid_spec=pltpu.PrefetchScalarGridSpec(
            num_scalar_prefetch=2,
            grid=(pair_dev // terms,),
            in_specs=[
                pl.BlockSpec(
                    (1, width, rows),
                    lambda g, m, x: (
                        jnp.bitwise_xor(within // pairs, jnp.bitwise_and(m[0], 1)) * pairs
                        + within % pairs, 0, 0
                    ),
                )
            ]
            + [part_spec(j) for j in range(terms)]
            + [left_spec(j) for j in range(terms)],
            out_specs=(out_spec, out_spec),
        ),
        cost_estimate=pl.CostEstimate(
            flops=2 * pair_dev * width * part * (rows + width),
            bytes_accessed=2 * pair_dev * rows * part,
            transcendentals=0,
        ),
        compiler_params=pltpu.CompilerParams(
            dimension_semantics=("arbitrary",), vmem_limit_bytes=40 << 20
        ),
        name="renorm",
    )(meta, idx, iso, *[parts] * terms, *[left_env] * terms)


def every_sector(block):
    for bit in range((lax.axis_size("sector") - 1).bit_length()):
        block = jnp.concatenate([block, from_partner(block, "sector", bit)], axis=0)
    return block


def add(a, b):
    return (a.astype(f32) + b.astype(f32)).astype(bf16)


def sum_terms(keep, send, slice_bits, all_bits):
    total = add(keep, from_partner(send, "term", 0))
    mine = add(total[0], from_partner(total[1], "term", slice_bits))
    others = list(range(slice_bits + 1, all_bits)) + list(range(1, slice_bits))
    for bit in others:
        mine = add(mine, from_partner(mine, "term", bit))
    return mine, from_partner(mine, "term", slice_bits)


def body(wave_in, left_env, right_env, shift_map, live_rows):
    sec_dev, rows, width = wave_in.shape
    pair_dev = left_env.shape[1]
    slices = rows // left_env.shape[3]
    part = rows // slices
    slice_bits = slices.bit_length() - 1
    positions = lax.axis_size("term")
    all_bits = positions.bit_length() - 1
    sectors = lax.axis_size("sector")
    me = lax.axis_index("term")
    my_sector = lax.axis_index("sector")
    own_slice = me % slices
    core = me % 2
    meta = jnp.reshape(me, (1,)).astype(jnp.int32)
    first_sector = my_sector * sec_dev
    terms_here = lax.dynamic_slice_in_dim(shift_map, (me // slices) * pair_dev, pair_dev, 0)
    sources = lax.dynamic_slice_in_dim(terms_here, first_sector, sec_dev, 1).T
    far_device = (sources // sec_dev) ^ my_sector
    sources = sources % sec_dev
    limits = lax.dynamic_slice_in_dim(live_rows, first_sector, sec_dev, 0)
    right = jnp.swapaxes(right_env, 2, 3)

    size = 2
    pairs = size // 2
    chunks = [(first, size) for first in range(0, sec_dev, size)]
    in_chunk = sources % size
    placed = (sources // size) * size + ((in_chunk // pairs) ^ core) * pairs + in_chunk % pairs
    wave_idx = far_device * sec_dev + sources
    part_idx = far_device * sec_dev + placed

    mine_rows = lax.dynamic_slice_in_dim(wave_in, own_slice * part, part, 1)
    every_rows = every_sector(mine_rows)
    near = from_partner(right, "term", 0)

    isos, own_rows, send_rows = [], [], []
    every_part = jnp.zeros((sectors, sec_dev, width, part), bf16)
    for first, count in chunks:
        blocks = {0: right, 1: near}
        own = lax.slice_in_dim(right, first, first + count, axis=0)
        for bit in range(1, slice_bits):
            known = [own] + [blocks[k] for k in range(2, 1 << bit, 2)]
            for k, block in zip(range(0, 1 << bit, 2), known):
                there = k | 1 << bit
                blocks[there] = from_partner(block, "term", bit)
                blocks[there + 1] = from_partner(blocks[there], "term", 0)
        starts = [first if k < 2 else 0 for k in range(slices)]
        keep, send = sigma_call(
            meta, wave_idx[first:first + count], every_rows, [blocks[k] for k in range(slices)],
            starts, left_env, first, count,
        )
        own, far = sum_terms(keep, send, slice_bits, all_bits)
        mine_limits = lax.dynamic_slice_in_dim(limits, first + core * pairs, pairs, 0)
        iso, iso_rows = update_call(meta, mine_limits, own, far, wave_in, first, slices, positions)
        iso = jnp.concatenate([iso, from_partner(iso, "term", 0)], axis=0)
        isos.append(iso)
        own_rows.append(iso_rows[0])
        send_rows.append(iso_rows[1])
        iso_part = lax.dynamic_slice_in_dim(iso, own_slice * part, part, 2)
        spread = every_sector(iso_part[None])
        every_part = lax.dynamic_update_slice(every_part, spread, (0, first, 0, 0))
    own_rows = jnp.stack(own_rows)
    far_rows = from_partner(jnp.stack(send_rows), "term", 0)
    lower = jnp.where(core == 0, own_rows, far_rows)
    upper = jnp.where(core == 0, far_rows, own_rows)
    wave_out = jnp.stack([lower, upper], axis=1).reshape(sec_dev, rows // positions, width)
    parts = every_part.reshape(sectors * sec_dev, width, part)

    share = width // slices
    env = jnp.zeros((sec_dev, pair_dev, share, width), bf16)
    for first in range(sec_dev):
        keep, send = renorm_call(
            meta, part_idx[first], isos[first // size], first % size, parts, left_env, first, slices
        )
        value = keep.astype(f32) + from_partner(send, "term", 0).astype(f32)
        value = value.reshape((2,) * (slice_bits - 1) + value.shape[1:])
        for bit in reversed(range(1, slice_bits)):
            value = value[0] + from_partner(value[1].astype(bf16), "term", bit).astype(f32)
        env = lax.dynamic_update_slice(env, value.astype(bf16), (first, 0, 0, 0))
    return wave_out, jnp.swapaxes(env, 2, 3)


def solution(mesh):
    in_specs = (
        P("sector", None, None),
        P("sector", "term", None, None),
        P("sector", "term", None, None),
        P(),
        P(),
    )
    out_specs = (P("sector", "term", None), P("sector", "term", None, None))

    return jax.shard_map(body, mesh=mesh, in_specs=in_specs, out_specs=out_specs, check_vma=False)
```

time: 716 us -> 419 us (0.59)
  waiting for transfers between devices: 442 us -> 197 us
  matrix products: 169 us -> 0 us
  Pallas kernels: 0 us -> 146 us
  starting transfers between devices: 5.66 us -> 47 us
  other arithmetic: 44.2 us -> 10.7 us
  local copies, waits for them, and re-layouts: 35.1 us -> 11.2 us
  between operations: 14.6 us -> 1.64 us
    dot_general x28 -> x0, matrix products: 169 us -> none  [the longest x1 30.8 us: body(): jnp.einsum('spia,spac->sic', left_env, operator_applied, preferred_elemen...]
    psum x1 -> x0, waiting for transfers between devices: 164 us -> none  [body(): sigma_block_sum = lax.psum(term_total, 'term')]
    pallas_call x0 -> x16, Pallas kernels: none -> 146 us  [the longest x8 66.5 us: renorm_call(): pl.pallas_call(functools.partial(renorm_kernel, slices, terms, 1 / math.s...]
    ppermute x4 -> x55, starting transfers between devices: 5.01 us -> 47 us  [from_partner(): return lax.ppermute(block, axis, route)]
    all_gather x2 -> x0, waiting for transfers between devices: 40.7 us -> none  [the longest x1 33.3 us: body(): every_rows = lax.all_gather(mine_rows, 'sector', axis=0, tiled=True)]
    ppermute x4 -> x55, waiting for transfers between devices: 237 us -> 197 us  [from_partner(): return lax.ppermute(block, axis, route)]
    gather x2 -> x0, local copies, waits for them, and re-layouts: 16.9 us -> none  [the longest x1 8.49 us: body(): picked_wave = every_source[sources]]
    convert_element_type x4 -> x17, other arithmetic: 17.7 us -> 1.51 us  [the longest x16 1.39 us: add(): return (a.astype(f32) + b.astype(f32)).astype(bf16)]
  transfers between devices with their start and end apart: 7 -> 55, of which waited for: 7 -> 27; matrix products, arithmetic and copies ran while one was open for 6% -> 5% of each run, Pallas kernels for 0% -> 33%
where the time goes in v1:
time: 419 us; the launch traced here: 414 us
  waiting for transfers between devices  197 us (47%)
  Pallas kernels  146 us (35%)
  starting transfers between devices  47 us (11%)
  local copies, waits for them, and re-layouts  11.2 us (3%)
  other arithmetic  10.7 us (3%)
    ppermute x55, waiting for transfers between devices, from_partner(): return lax.ppermute(block, axis, route)  197 us
    pallas_call x8, Pallas kernels, renorm_call(): pl.pallas_call(functools.partial(renorm_kernel, slices, terms, 1 / math.s...  66.5 us
    pallas_call x4, Pallas kernels, sigma_call(): pl.pallas_call(functools.partial(sigma_kernel, len(rights), terms), out_s...  50.4 us
    ppermute x55, starting transfers between devices, from_partner(): return lax.ppermute(block, axis, route)  47 us
    pallas_call x4, Pallas kernels, update_call(): pl.pallas_call(functools.partial(update_kernel, slices, each), out_shape=...  29.1 us
  transfers between devices with their start and end apart: 55, of which 27 were waited for; matrix products, arithmetic and copies ran while one was open for 5% of the time, Pallas kernels for 33%

profile of v1, /device:TPU:0, one launch (start us, length us, event | category | flops | bytes accessed | tf_op | source)
XLA Modules:
  0.0 414.0 jit_solution(16125514094067677404)
XLA Ops:
  13.1 12.9 %collective-permute-done.23.refs_5_ = bf16[2,12,64,256]{3,2,1,0:T(8,128)(2,1)} collective-permute-done((bf16[2,12,64,256]{3,2,1,0:T(8,128)(2,1)}, bf16[2,12,64,256]{3,2,1,0:T(8,128)(2,1)}, u32[]{:S(2)}, u32[]{:S(2)}) %collective-permute-start.23) | collective-permute-done | bytes 786464 | tf_op jit(solution)/shard_map/ppermute | solution.py:27
  28.0 14.8 %collective-permute-done.16.refs_5_ = bf16[2,12,64,256]{3,2,1,0:T(8,128)(2,1)} collective-permute-done((bf16[2,12,64,256]{3,2,1,0:T(8,128)(2,1)}, bf16[2,12,64,256]{3,2,1,0:T(8,128)(2,1)}, u32[]{:S(2)}, u32[]{:S(2)}) %collective-permute-start.16) | collective-permute-done | bytes 786464 | tf_op jit(solution)/shard_map/ppermute | solution.py:27
  42.9 16.8 %collective-permute-done.9.refs_5_ = bf16[2,12,64,256]{3,2,1,0:T(8,128)(2,1)} collective-permute-done((bf16[2,12,64,256]{3,2,1,0:T(8,128)(2,1)}, bf16[2,12,64,256]{3,2,1,0:T(8,128)(2,1)}, u32[]{:S(2)}, u32[]{:S(2)}) %collective-permute-start.9) | collective-permute-done | bytes 786464 | tf_op jit(solution)/shard_map/ppermute | solution.py:27
  60.4 15.9 %collective-permute-done.2.refs_5_ = bf16[2,12,64,256]{3,2,1,0:T(8,128)(2,1)} collective-permute-done((bf16[2,12,64,256]{3,2,1,0:T(8,128)(2,1)}, bf16[2,12,64,256]{3,2,1,0:T(8,128)(2,1)}, u32[]{:S(2)}, u32[]{:S(2)}) %collective-permute-start.2) | collective-permute-done | bytes 786464 | tf_op jit(solution)/shard_map/ppermute | solution.py:27
  78.6 12.6 %sigma.7 = (bf16[2,1,512,256]{3,2,1,0:T(8,128)(2,1)S(1)}, bf16[2,1,512,256]{3,2,1,0:T(8,128)(2,1)S(1)}) custom-call(s32[1]{0:T(128)} %bitcast.meta, s32[2,12]{1,0:T(2,128)S(1)} %get-tuple-element.81.idx, bf16[16,256,256]{2,1,0:T(8,128)(2,1)S(1)} %pad_maximum_fusion.refs_0_.refs_1_.refs_2_, bf16[16,256,256]{2,1,0:T(8,128)(2,1)S(1)} %pad_maximum_fusion.refs_0_.refs_1_.refs_2_, ...), custom_call_target="tpu_custom_call" | custom-call | flops 4026531840 | bytes 12582912 | tf_op jit(solution)/shard_map/sigma/pallas_call | solution.py:119
  91.3 12.6 %sigma.6 = (bf16[2,1,512,256]{3,2,1,0:T(8,128)(2,1)S(1)}, bf16[2,1,512,256]{3,2,1,0:T(8,128)(2,1)S(1)}) custom-call(s32[1]{0:T(128)} %bitcast.meta, s32[2,12]{1,0:T(2,128)S(1)} %get-tuple-element.82.idx, bf16[16,256,256]{2,1,0:T(8,128)(2,1)S(1)} %pad_maximum_fusion.refs_0_.refs_1_.refs_2_, bf16[16,256,256]{2,1,0:T(8,128)(2,1)S(1)} %pad_maximum_fusion.refs_0_.refs_1_.refs_2_, ...), custom_call_target="tpu_custom_call" | custom-call | flops 4026531840 | bytes 12582912 | tf_op jit(solution)/shard_map/sigma/pallas_call | solution.py:119
  104.4 12.4 %sigma.5 = (bf16[2,1,512,256]{3,2,1,0:T(8,128)(2,1)S(1)}, bf16[2,1,512,256]{3,2,1,0:T(8,128)(2,1)S(1)}) custom-call(s32[1]{0:T(128)} %bitcast.meta, s32[2,12]{1,0:T(2,128)S(1)} %get-tuple-element.83.idx, bf16[16,256,256]{2,1,0:T(8,128)(2,1)S(1)} %pad_maximum_fusion.refs_0_.refs_1_.refs_2_, bf16[16,256,256]{2,1,0:T(8,128)(2,1)S(1)} %pad_maximum_fusion.refs_0_.refs_1_.refs_2_, ...), custom_call_target="tpu_custom_call" | custom-call | flops 4026531840 | bytes 12582912 | tf_op jit(solution)/shard_map/sigma/pallas_call | solution.py:119
  116.9 12.8 %sigma.4 = (bf16[2,1,512,256]{3,2,1,0:T(8,128)(2,1)S(1)}, bf16[2,1,512,256]{3,2,1,0:T(8,128)(2,1)S(1)}) custom-call(s32[1]{0:T(128)} %bitcast.meta, s32[2,12]{1,0:T(2,128)S(1)} %get-tuple-element.80.idx, bf16[16,256,256]{2,1,0:T(8,128)(2,1)S(1)} %pad_maximum_fusion.refs_0_.refs_1_.refs_2_, bf16[16,256,256]{2,1,0:T(8,128)(2,1)S(1)} %pad_maximum_fusion.refs_0_.refs_1_.refs_2_, ...), custom_call_target="tpu_custom_call" | custom-call | flops 4026531840 | bytes 12582912 | tf_op jit(solution)/shard_map/sigma/pallas_call | solution.py:119
  142.7 8.3 %collective-permute-done.19 = bf16[1,512,256]{2,1,0:T(8,128)(2,1)S(1)} collective-permute-done((bf16[1,512,256]{2,1,0:T(8,128)(2,1)S(1)}, bf16[1,512,256]{2,1,0:T(8,128)(2,1)S(1)}, u32[]{:S(2)}, u32[]{:S(2)}) %collective-permute-start.19) | collective-permute-done | bytes 262176 | tf_op jit(solution)/shard_map/ppermute | solution.py:27
  153.0 8.5 %collective-permute-done.12 = bf16[1,512,256]{2,1,0:T(8,128)(2,1)S(1)} collective-permute-done((bf16[1,512,256]{2,1,0:T(8,128)(2,1)S(1)}, bf16[1,512,256]{2,1,0:T(8,128)(2,1)S(1)}, u32[]{:S(2)}, u32[]{:S(2)}) %collective-permute-start.12) | collective-permute-done | bytes 262176 | tf_op jit(solution)/shard_map/ppermute | solution.py:27
  168.3 13.5 %collective-permute-done.20 = bf16[1,512,256]{2,1,0:T(8,128)(2,1)S(1)} collective-permute-done((bf16[1,512,256]{2,1,0:T(8,128)(2,1)S(1)}, bf16[1,512,256]{2,1,0:T(8,128)(2,1)S(1)}, u32[]{:S(2)}, u32[]{:S(2)}) %collective-permute-start.20) | collective-permute-done | bytes 262176 | tf_op jit(solution)/shard_map/ppermute | solution.py:27
  268.7 8.6 %renorm.8 = (bf16[2,1,12,64,256]{4,3,2,1,0:T(8,128)(2,1)S(1)}, bf16[2,1,12,64,256]{4,3,2,1,0:T(8,128)(2,1)}) custom-call(s32[1]{0:T(128)} %bitcast.meta, s32[12]{0:T(128)S(1)} %get-tuple-element.79.idx, bf16[2,256,1024]{2,1,0:T(8,128)(2,1)S(1)} %constant_dynamic-update-slice_fusion.iso_ref, bf16[16,256,256]{2,1,0:T(8,128)(2,1)S(1)} %bitcast.179, ...), custom_call_target="tpu_custom_call" | custom-call | flops 2013265920 | bytes 6291456 | tf_op jit(solution)/shard_map/renorm/pallas_call | solution.py:281
  277.3 8.6 %renorm.9 = (bf16[2,1,12,64,256]{4,3,2,1,0:T(8,128)(2,1)S(1)}, bf16[2,1,12,64,256]{4,3,2,1,0:T(8,128)(2,1)}) custom-call(s32[1]{0:T(128)} %bitcast.meta, s32[12]{0:T(128)S(1)} %get-tuple-element.78.idx, bf16[2,256,1024]{2,1,0:T(8,128)(2,1)S(1)} %constant_dynamic-update-slice_fusion.iso_ref, bf16[16,256,256]{2,1,0:T(8,128)(2,1)S(1)} %bitcast.182, ...), custom_call_target="tpu_custom_call" | custom-call | flops 2013265920 | bytes 6291456 | tf_op jit(solution)/shard_map/renorm/pallas_call | solution.py:281
  286.4 8.8 %renorm.10 = (bf16[2,1,12,64,256]{4,3,2,1,0:T(8,128)(2,1)S(1)}, bf16[2,1,12,64,256]{4,3,2,1,0:T(8,128)(2,1)}) custom-call(s32[1]{0:T(128)} %bitcast.meta, s32[12]{0:T(128)S(1)} %get-tuple-element.77.idx, bf16[2,256,1024]{2,1,0:T(8,128)(2,1)S(1)} %constant_dynamic-update-slice_fusion.2.iso_ref, bf16[16,256,256]{2,1,0:T(8,128)(2,1)S(1)} %bitcast.185, ...), custom_call_target="tpu_custom_call" | custom-call | flops 2013265920 | bytes 6291456 | tf_op jit(solution)/shard_map/renorm/pallas_call | solution.py:281
  295.2 8.6 %renorm.11 = (bf16[2,1,12,64,256]{4,3,2,1,0:T(8,128)(2,1)S(1)}, bf16[2,1,12,64,256]{4,3,2,1,0:T(8,128)(2,1)}) custom-call(s32[1]{0:T(128)} %bitcast.meta, s32[12]{0:T(128)S(1)} %get-tuple-element.76.idx, bf16[2,256,1024]{2,1,0:T(8,128)(2,1)S(1)} %constant_dynamic-update-slice_fusion.2.iso_ref, bf16[16,256,256]{2,1,0:T(8,128)(2,1)S(1)} %bitcast.190, ...), custom_call_target="tpu_custom_call" | custom-call | flops 2013265920 | bytes 6291456 | tf_op jit(solution)/shard_map/renorm/pallas_call | solution.py:281
  304.3 8.0 %renorm.12 = (bf16[2,1,12,64,256]{4,3,2,1,0:T(8,128)(2,1)S(1)}, bf16[2,1,12,64,256]{4,3,2,1,0:T(8,128)(2,1)S(1)}) custom-call(s32[1]{0:T(128)} %bitcast.meta, s32[12]{0:T(128)S(1)} %get-tuple-element.75.idx, bf16[2,256,1024]{2,1,0:T(8,128)(2,1)S(1)} %copy-done.2, bf16[16,256,256]{2,1,0:T(8,128)(2,1)S(1)} %bitcast.191, bf16[16,256,256]{2,1,0:T(8,128)(2,1)S(1)} %bitcast.192, ...), custom_call_target="tpu_custom_call" | custom-call | flops 2013265920 | bytes 6291456 | tf_op jit(solution)/shard_map/renorm/pallas_call | solution.py:281
  312.4 8.0 %renorm.13 = (bf16[2,1,12,64,256]{4,3,2,1,0:T(8,128)(2,1)S(1)}, bf16[2,1,12,64,256]{4,3,2,1,0:T(8,128)(2,1)S(1)}) custom-call(s32[1]{0:T(128)} %bitcast.meta, s32[12]{0:T(128)S(1)} %get-tuple-element.74.idx, bf16[2,256,1024]{2,1,0:T(8,128)(2,1)S(1)} %copy-done.2, bf16[16,256,256]{2,1,0:T(8,128)(2,1)S(1)} %bitcast.194, bf16[16,256,256]{2,1,0:T(8,128)(2,1)S(1)} %bitcast.195, ...), custom_call_target="tpu_custom_call" | custom-call | flops 2013265920 | bytes 6291456 | tf_op jit(solution)/shard_map/renorm/pallas_call | solution.py:281
  320.4 8.0 %renorm.14 = (bf16[2,1,12,64,256]{4,3,2,1,0:T(8,128)(2,1)S(1)}, bf16[2,1,12,64,256]{4,3,2,1,0:T(8,128)(2,1)S(1)}) custom-call(s32[1]{0:T(128)} %bitcast.meta, s32[12]{0:T(128)S(1)} %get-tuple-element.73.idx, bf16[2,256,1024]{2,1,0:T(8,128)(2,1)S(1)} %copy-done.4, bf16[16,256,256]{2,1,0:T(8,128)(2,1)S(1)} %bitcast.197, bf16[16,256,256]{2,1,0:T(8,128)(2,1)S(1)} %bitcast.198, ...), custom_call_target="tpu_custom_call" | custom-call | flops 2013265920 | bytes 6291456 | tf_op jit(solution)/shard_map/renorm/pallas_call | solution.py:281
  328.4 8.0 %renorm.15 = (bf16[2,1,12,64,256]{4,3,2,1,0:T(8,128)(2,1)S(1)}, bf16[2,1,12,64,256]{4,3,2,1,0:T(8,128)(2,1)S(1)}) custom-call(s32[1]{0:T(128)} %bitcast.meta, s32[12]{0:T(128)S(1)} %get-tuple-element.72.idx, bf16[2,256,1024]{2,1,0:T(8,128)(2,1)S(1)} %copy-done.4, bf16[16,256,256]{2,1,0:T(8,128)(2,1)S(1)} %bitcast.200, bf16[16,256,256]{2,1,0:T(8,128)(2,1)S(1)} %bitcast.201, ...), custom_call_target="tpu_custom_call" | custom-call | flops 2013265920 | bytes 6291456 | tf_op jit(solution)/shard_map/renorm/pallas_call | solution.py:281
  363.0 7.8 %collective-permute-done.44 = bf16[1,12,64,256]{3,2,1,0:T(8,128)(2,1)S(1)} collective-permute-done((bf16[1,12,64,256]{3,2,1,0:T(8,128)(2,1)S(1)}, bf16[1,12,64,256]{3,2,1,0:T(8,128)(2,1)S(1)}, u32[]{:S(2)}, u32[]{:S(2)}) %collective-permute-start.44) | collective-permute-done | bytes 393248 | tf_op jit(solution)/shard_map/ppermute | solution.py:27
  371.4 7.8 %collective-permute-done.46 = bf16[1,12,64,256]{3,2,1,0:T(8,128)(2,1)S(1)} collective-permute-done((bf16[1,12,64,256]{3,2,1,0:T(8,128)(2,1)S(1)}, bf16[1,12,64,256]{3,2,1,0:T(8,128)(2,1)S(1)}, u32[]{:S(2)}, u32[]{:S(2)}) %collective-permute-start.46) | collective-permute-done | bytes 393248 | tf_op jit(solution)/shard_map/ppermute | solution.py:27
  379.3 8.3 %collective-permute-done.48 = bf16[1,12,64,256]{3,2,1,0:T(8,128)(2,1)S(1)} collective-permute-done((bf16[1,12,64,256]{3,2,1,0:T(8,128)(2,1)S(1)}, bf16[1,12,64,256]{3,2,1,0:T(8,128)(2,1)S(1)}, u32[]{:S(2)}, u32[]{:S(2)}) %collective-permute-start.48) | collective-permute-done | bytes 393248 | tf_op jit(solution)/shard_map/ppermute | solution.py:27
  387.7 8.3 %collective-permute-done.50 = bf16[1,12,64,256]{3,2,1,0:T(8,128)(2,1)S(1)} collective-permute-done((bf16[1,12,64,256]{3,2,1,0:T(8,128)(2,1)S(1)}, bf16[1,12,64,256]{3,2,1,0:T(8,128)(2,1)S(1)}, u32[]{:S(2)}, u32[]{:S(2)}) %collective-permute-start.50) | collective-permute-done | bytes 393248 | tf_op jit(solution)/shard_map/ppermute | solution.py:27
  396.2 8.3 %collective-permute-done.52 = bf16[1,12,64,256]{3,2,1,0:T(8,128)(2,1)S(1)} collective-permute-done((bf16[1,12,64,256]{3,2,1,0:T(8,128)(2,1)S(1)}, bf16[1,12,64,256]{3,2,1,0:T(8,128)(2,1)S(1)}, u32[]{:S(2)}, u32[]{:S(2)}) %collective-permute-start.52) | collective-permute-done | bytes 393248 | tf_op jit(solution)/shard_map/ppermute | solution.py:27
  (201 shorter events, 164.1 us)
Async XLA Ops:
  0.6 78.0 %collective-permute-start.1 = (bf16[8,12,64,256]{3,2,1,0:T(8,128)(2,1)}, bf16[8,12,64,256]{3,2,1,0:T(8,128)(2,1)S(1)}, u32[]{:S(2)}, u32[]{:S(2)}) collective-permute-start(bf16[8,12,64,256]{3,2,1,0:T(8,128)(2,1)} %bitcast.203), channel_id=1, source_target_pairs={{0,1},{1,0},{2,3},{3,2},{4,5},{5,4},{6,7},{7,6},{8,9},{9,8},{10,11... | collective-permute-start | bytes 9437192 | tf_op jit(solution)/shard_map/ppermute | solution.py:27
  7.3 35.6 %collective-permute-start.16 = (bf16[2,12,64,256]{3,2,1,0:T(8,128)(2,1)}, bf16[2,12,64,256]{3,2,1,0:T(8,128)(2,1)}, u32[]{:S(2)}, u32[]{:S(2)}) collective-permute-start(bf16[2,12,64,256]{3,2,1,0:T(8,128)(2,1)} %get-tuple-element.68), channel_id=1, source_target_pairs={{0,2},{2,0},{1,3},{3,1},{4,6},{6,4},{5,7},{7,5},{8,10},{10,8},{9,1... | collective-permute-start | bytes 2359304 | tf_op jit(solution)/shard_map/ppermute | solution.py:27
  7.3 52.3 %collective-permute-start.9 = (bf16[2,12,64,256]{3,2,1,0:T(8,128)(2,1)}, bf16[2,12,64,256]{3,2,1,0:T(8,128)(2,1)}, u32[]{:S(2)}, u32[]{:S(2)}) collective-permute-start(bf16[2,12,64,256]{3,2,1,0:T(8,128)(2,1)} %get-tuple-element.69), channel_id=1, source_target_pairs={{0,2},{2,0},{1,3},{3,1},{4,6},{6,4},{5,7},{7,5},{8,10},{10,8},{9,1... | collective-permute-start | bytes 2359304 | tf_op jit(solution)/shard_map/ppermute | solution.py:27
  11.5 64.8 %collective-permute-start = (bf16[8,256,256]{2,1,0:T(8,128)(2,1)}, bf16[8,256,256]{2,1,0:T(8,128)(2,1)}, u32[]{:S(2)}, u32[]{:S(2)}) collective-permute-start(bf16[8,256,256]{2,1,0:T(8,128)(2,1)} %constant_dynamic-slice_fusion), channel_id=1, source_target_pairs={{0,16},{16,0},{1,17},{17,1},{2,18},{18,2},{3,19},{19,3},{4,20},{20... | collective-permute-start | bytes 3145736 | tf_op jit(solution)/shard_map/ppermute | solution.py:27
  26.0 50.4 %collective-permute-start.2 = (bf16[2,12,64,256]{3,2,1,0:T(8,128)(2,1)}, bf16[2,12,64,256]{3,2,1,0:T(8,128)(2,1)}, u32[]{:S(2)}, u32[]{:S(2)}) collective-permute-start(bf16[2,12,64,256]{3,2,1,0:T(8,128)(2,1)} %get-tuple-element.66), channel_id=1, source_target_pairs={{0,2},{2,0},{1,3},{3,1},{4,6},{6,4},{5,7},{7,5},{8,10},{10,8},{9,1... | collective-permute-start | bytes 2359304 | tf_op jit(solution)/shard_map/ppermute | solution.py:27
  42.8 35.8 %collective-permute-start.24 = (bf16[2,12,64,256]{3,2,1,0:T(8,128)(2,1)}, bf16[2,12,64,256]{3,2,1,0:T(8,128)(2,1)}, u32[]{:S(2)}, u32[]{:S(2)}) collective-permute-start(bf16[2,12,64,256]{3,2,1,0:T(8,128)(2,1)} %collective-permute-done.23.refs_5_), channel_id=1, source_target_pairs={{0,1},{1,0},{2,3},{3,2},{4,5},{5,4},{6,7},{7,6},{8,9},{9,8},{10,11... | collective-permute-start | bytes 2359304 | tf_op jit(solution)/shard_map/ppermute | solution.py:27
  59.7 31.6 %collective-permute-start.17 = (bf16[2,12,64,256]{3,2,1,0:T(8,128)(2,1)}, bf16[2,12,64,256]{3,2,1,0:T(8,128)(2,1)}, u32[]{:S(2)}, u32[]{:S(2)}) collective-permute-start(bf16[2,12,64,256]{3,2,1,0:T(8,128)(2,1)} %collective-permute-done.16.refs_5_), channel_id=1, source_target_pairs={{0,1},{1,0},{2,3},{3,2},{4,5},{5,4},{6,7},{7,6},{8,9},{9,8},{10,11... | collective-permute-start | bytes 2359304 | tf_op jit(solution)/shard_map/ppermute | solution.py:27
  76.3 40.6 %collective-permute-start.3 = (bf16[2,12,64,256]{3,2,1,0:T(8,128)(2,1)}, bf16[2,12,64,256]{3,2,1,0:T(8,128)(2,1)S(1)}, u32[]{:S(2)}, u32[]{:S(2)}) collective-permute-start(bf16[2,12,64,256]{3,2,1,0:T(8,128)(2,1)} %collective-permute-done.2.refs_5_), channel_id=1, source_target_pairs={{0,1},{1,0},{2,3},{3,2},{4,5},{5,4},{6,7},{7,6},{8,9},{9,8},{10,11... | collective-permute-start | bytes 2359304 | tf_op jit(solution)/shard_map/ppermute | solution.py:27
  91.2 39.1 %collective-permute-start.25 = (bf16[2,1,512,256]{3,2,1,0:T(8,128)(2,1)S(1)}, bf16[2,1,512,256]{3,2,1,0:T(8,128)(2,1)S(1)}, u32[]{:S(2)}, u32[]{:S(2)}) collective-permute-start(bf16[2,1,512,256]{3,2,1,0:T(8,128)(2,1)S(1)} %get-tuple-element.44), channel_id=1, source_target_pairs={{0,1},{1,0},{2,3},{3,2},{4,5},{5,4},{6,7},{7,6},{8,9},{9,8},{10,11... | collective-permute-start | bytes 1572872 | tf_op jit(solution)/shard_map/ppermute | solution.py:27
  133.0 28.6 %collective-permute-start.12 = (bf16[1,512,256]{2,1,0:T(8,128)(2,1)S(1)}, bf16[1,512,256]{2,1,0:T(8,128)(2,1)S(1)}, u32[]{:S(2)}, u32[]{:S(2)}) collective-permute-start(bf16[1,512,256]{2,1,0:T(8,128)(2,1)S(1)} %slice_bitcast_fusion.12), channel_id=1, source_target_pairs={{0,4},{4,0},{1,5},{5,1},{2,6},{6,2},{3,7},{7,3},{8,12},{12,8},{9,1... | collective-permute-start | bytes 786440 | tf_op jit(solution)/shard_map/ppermute | solution.py:27
  135.1 31.3 %collective-permute-start.5 = (bf16[1,512,256]{2,1,0:T(8,128)(2,1)S(1)}, bf16[1,512,256]{2,1,0:T(8,128)(2,1)S(1)}, u32[]{:S(2)}, u32[]{:S(2)}) collective-permute-start(bf16[1,512,256]{2,1,0:T(8,128)(2,1)S(1)} %slice_bitcast_fusion.14), channel_id=1, source_target_pairs={{0,4},{4,0},{1,5},{5,1},{2,6},{6,2},{3,7},{7,3},{8,12},{12,8},{9,1... | collective-permute-start | bytes 786440 | tf_op jit(solution)/shard_map/ppermute | solution.py:27
  151.0 30.8 %collective-permute-start.20 = (bf16[1,512,256]{2,1,0:T(8,128)(2,1)S(1)}, bf16[1,512,256]{2,1,0:T(8,128)(2,1)S(1)}, u32[]{:S(2)}, u32[]{:S(2)}) collective-permute-start(bf16[1,512,256]{2,1,0:T(8,128)(2,1)S(1)} %fusion.20), channel_id=1, source_target_pairs={{0,8},{8,0},{1,9},{9,1},{2,10},{10,2},{3,11},{11,3},{4,12},{12,4},... | collective-permute-start | bytes 786440 | tf_op jit(solution)/shard_map/ppermute | solution.py:27
  195.1 38.7 %collective-permute-start.22 = (bf16[1,512,256]{2,1,0:T(8,128)(2,1)S(1)}, bf16[1,512,256]{2,1,0:T(8,128)(2,1)S(1)}, u32[]{:S(2)}, u32[]{:S(2)}) collective-permute-start(bf16[1,512,256]{2,1,0:T(8,128)(2,1)S(1)} %add_convert_fusion.6.own_ref), channel_id=1, source_target_pairs={{0,4},{4,0},{1,5},{5,1},{2,6},{6,2},{3,7},{7,3},{8,12},{12,8},{9,1... | collective-permute-start | bytes 786440 | tf_op jit(solution)/shard_map/ppermute | solution.py:27
  196.5 29.2 %collective-permute-start.15 = (bf16[1,512,256]{2,1,0:T(8,128)(2,1)S(1)}, bf16[1,512,256]{2,1,0:T(8,128)(2,1)S(1)}, u32[]{:S(2)}, u32[]{:S(2)}) collective-permute-start(bf16[1,512,256]{2,1,0:T(8,128)(2,1)S(1)} %add_convert_fusion.8.own_ref), channel_id=1, source_target_pairs={{0,4},{4,0},{1,5},{5,1},{2,6},{6,2},{3,7},{7,3},{8,12},{12,8},{9,1... | collective-permute-start | bytes 786440 | tf_op jit(solution)/shard_map/ppermute | solution.py:27
  277.3 59.1 %collective-permute-start.39 = (bf16[2,1,12,64,256]{4,3,2,1,0:T(8,128)(2,1)}, bf16[2,1,12,64,256]{4,3,2,1,0:T(8,128)(2,1)}, u32[]{:S(2)}, u32[]{:S(2)}) collective-permute-start(bf16[2,1,12,64,256]{4,3,2,1,0:T(8,128)(2,1)} %get-tuple-element.51), channel_id=1, source_target_pairs={{0,1},{1,0},{2,3},{3,2},{4,5},{5,4},{6,7},{7,6},{8,9},{9,8},{10,11... | collective-permute-start | bytes 2359304 | tf_op jit(solution)/shard_map/ppermute | solution.py:27
  285.9 52.4 %collective-permute-start.41 = (bf16[2,1,12,64,256]{4,3,2,1,0:T(8,128)(2,1)}, bf16[2,1,12,64,256]{4,3,2,1,0:T(8,128)(2,1)}, u32[]{:S(2)}, u32[]{:S(2)}) collective-permute-start(bf16[2,1,12,64,256]{4,3,2,1,0:T(8,128)(2,1)} %get-tuple-element.53), channel_id=1, source_target_pairs={{0,1},{1,0},{2,3},{3,2},{4,5},{5,4},{6,7},{7,6},{8,9},{9,8},{10,11... | collective-permute-start | bytes 2359304 | tf_op jit(solution)/shard_map/ppermute | solution.py:27
  295.2 44.6 %collective-permute-start.43 = (bf16[2,1,12,64,256]{4,3,2,1,0:T(8,128)(2,1)}, bf16[2,1,12,64,256]{4,3,2,1,0:T(8,128)(2,1)}, u32[]{:S(2)}, u32[]{:S(2)}) collective-permute-start(bf16[2,1,12,64,256]{4,3,2,1,0:T(8,128)(2,1)} %get-tuple-element.55), channel_id=1, source_target_pairs={{0,1},{1,0},{2,3},{3,2},{4,5},{5,4},{6,7},{7,6},{8,9},{9,8},{10,11... | collective-permute-start | bytes 2359304 | tf_op jit(solution)/shard_map/ppermute | solution.py:27
  303.8 38.1 %collective-permute-start.45 = (bf16[2,1,12,64,256]{4,3,2,1,0:T(8,128)(2,1)}, bf16[2,1,12,64,256]{4,3,2,1,0:T(8,128)(2,1)}, u32[]{:S(2)}, u32[]{:S(2)}) collective-permute-start(bf16[2,1,12,64,256]{4,3,2,1,0:T(8,128)(2,1)} %get-tuple-element.57), channel_id=1, source_target_pairs={{0,1},{1,0},{2,3},{3,2},{4,5},{5,4},{6,7},{7,6},{8,9},{9,8},{10,11... | collective-permute-start | bytes 2359304 | tf_op jit(solution)/shard_map/ppermute | solution.py:27
  312.3 31.5 %collective-permute-start.47 = (bf16[2,1,12,64,256]{4,3,2,1,0:T(8,128)(2,1)S(1)}, bf16[2,1,12,64,256]{4,3,2,1,0:T(8,128)(2,1)S(1)}, u32[]{:S(2)}, u32[]{:S(2)}) collective-permute-start(bf16[2,1,12,64,256]{4,3,2,1,0:T(8,128)(2,1)S(1)} %get-tuple-element.59), channel_id=1, source_target_pairs={{0,1},{1,0},{2,3},{3,2},{4,5},{5,4},{6,7},{7,6},{8,9},{9,8},{10,11... | collective-permute-start | bytes 2359304 | tf_op jit(solution)/shard_map/ppermute | solution.py:27
  346.6 32.6 %collective-permute-start.46 = (bf16[1,12,64,256]{3,2,1,0:T(8,128)(2,1)S(1)}, bf16[1,12,64,256]{3,2,1,0:T(8,128)(2,1)S(1)}, u32[]{:S(2)}, u32[]{:S(2)}) collective-permute-start(bf16[1,12,64,256]{3,2,1,0:T(8,128)(2,1)S(1)} %fusion.29), channel_id=1, source_target_pairs={{0,2},{2,0},{1,3},{3,1},{4,6},{6,4},{5,7},{7,5},{8,10},{10,8},{9,1... | collective-permute-start | bytes 1179656 | tf_op jit(solution)/shard_map/ppermute | solution.py:27
  348.4 39.2 %collective-permute-start.48 = (bf16[1,12,64,256]{3,2,1,0:T(8,128)(2,1)S(1)}, bf16[1,12,64,256]{3,2,1,0:T(8,128)(2,1)S(1)}, u32[]{:S(2)}, u32[]{:S(2)}) collective-permute-start(bf16[1,12,64,256]{3,2,1,0:T(8,128)(2,1)S(1)} %fusion.31), channel_id=1, source_target_pairs={{0,2},{2,0},{1,3},{3,1},{4,6},{6,4},{5,7},{7,5},{8,10},{10,8},{9,1... | collective-permute-start | bytes 1179656 | tf_op jit(solution)/shard_map/ppermute | solution.py:27
  353.9 42.1 %collective-permute-start.50 = (bf16[1,12,64,256]{3,2,1,0:T(8,128)(2,1)S(1)}, bf16[1,12,64,256]{3,2,1,0:T(8,128)(2,1)S(1)}, u32[]{:S(2)}, u32[]{:S(2)}) collective-permute-start(bf16[1,12,64,256]{3,2,1,0:T(8,128)(2,1)S(1)} %fusion.33), channel_id=1, source_target_pairs={{0,2},{2,0},{1,3},{3,1},{4,6},{6,4},{5,7},{7,5},{8,10},{10,8},{9,1... | collective-permute-start | bytes 1179656 | tf_op jit(solution)/shard_map/ppermute | solution.py:27
  362.3 42.1 %collective-permute-start.52 = (bf16[1,12,64,256]{3,2,1,0:T(8,128)(2,1)S(1)}, bf16[1,12,64,256]{3,2,1,0:T(8,128)(2,1)S(1)}, u32[]{:S(2)}, u32[]{:S(2)}) collective-permute-start(bf16[1,12,64,256]{3,2,1,0:T(8,128)(2,1)S(1)} %fusion.35), channel_id=1, source_target_pairs={{0,2},{2,0},{1,3},{3,1},{4,6},{6,4},{5,7},{7,5},{8,10},{10,8},{9,1... | collective-permute-start | bytes 1179656 | tf_op jit(solution)/shard_map/ppermute | solution.py:27
  370.8 41.2 %collective-permute-start.54 = (bf16[1,12,64,256]{3,2,1,0:T(8,128)(2,1)S(1)}, bf16[1,12,64,256]{3,2,1,0:T(8,128)(2,1)S(1)}, u32[]{:S(2)}, u32[]{:S(2)}) collective-permute-start(bf16[1,12,64,256]{3,2,1,0:T(8,128)(2,1)S(1)} %fusion.37), channel_id=1, source_target_pairs={{0,2},{2,0},{1,3},{3,1},{4,6},{6,4},{5,7},{7,5},{8,10},{10,8},{9,1... | collective-permute-start | bytes 1179656 | tf_op jit(solution)/shard_map/ppermute | solution.py:27
  (40 other events, 623.6 us)
